TPU v7x, 256 devices: a whole 4x4x8 slice. The times are simulated.
256 devices in a mesh: lat: 16 (over y, x_lo, core), lon: 16 (over z, x_hi).
Axes of the slice: x: 4 (x_hi: 2, x_lo: 2; x = x_hi * 2 + x_lo), y: 4, z: 8, core: 2. Of those that a mesh axis runs over, the one named last changes fastest.
Arguments:
- adjoint: float32 [8, 8, 512, 2048], P(None, None, 'lat', 'lon'), may hold values from -6 to 6
- transport: float32 [6, 8, 512, 2048], P(None, None, 'lat', 'lon'), may hold values from 0.03 to 0.14
- cell_weight: float32 [512, 2048], P('lat', 'lon'), may hold values from 0.1 to 1
- region_local: int32 [512, 2048], P('lat', 'lon'), may hold values from 0 to 255
- tile_regions: int32 [256, 256], replicated, may hold values from 0 to 16383, as said below
- polar_rows: int32 [512], P('lat'), may hold values 0 or 1
- week_index: int32 [1], replicated, may hold values from 0 to 51
- grad_in: bfloat16 [16384, 416], P(('lat', 'lon')), may hold values from -6 to 6
- covariance: bfloat16 [16384, 16384], P(('lat', 'lon')), may hold values from -0.1875 to 0.1875
Outputs:
- adjoint_out: float32 [8, 8, 512, 2048], P(None, None, 'lat', 'lon')
- precond: float32 [16384, 416], P(('lat', 'lon'))
Inputs may be any that keep to these rules, and one draw needn't show every extreme that they name: `tile_regions`: each row holds 256 different region numbers; with per = 1, entries o * per to o * per + per - 1 of a row lie in regions o * 64 to o * 64 + 63, for every o.
All inputs are finite; a program needn't handle non-finite values. No bound on the sum of `polar_rows` on one device may be relied on, other than what follows from the above.
Results may differ from a plain program's by a relative error of at most 0.00066.
Values may be sent and summed in bfloat16 or wider, within the bound.
A program may use at most 128 MiB of HBM per device.

v0:
```python
import functools
import jax
import jax.numpy as jnp
from jax import lax
from jax.sharding import Mesh
from jax.sharding import PartitionSpec as P

LON = ("lon_0", "lon_1")
LAT_LON = ("lat", "lon_0", "lon_1")


def extended_2(x, sides, width):
    for axis, dim in sides:
        size, length = (lax.axis_size(axis), x.shape[dim])
        up = [(i, (i + 1) % size) for i in range(size)]
        down = [(j, i) for i, j in up]
        last = lax.slice_in_dim(x, length - width, length, axis=dim)
        leading = lax.slice_in_dim(x, 0, width, axis=dim)
        before = lax.ppermute(last, axis, up)
        after = lax.ppermute(leading, axis, down)
        x = jnp.concatenate([before, x, after], axis=dim)
    return x


def one_axis_at_a_time(x, axes):
    return functools.reduce(lax.psum, axes, x)


def advance(padded, rates):
    centre = padded[:, :, 1:-1, 1:-1]
    to_east = padded[:, :, 1:-1, 2:] - centre
    to_west = padded[:, :, 1:-1, :-2] - centre
    to_north = padded[:, :, 2:, 1:-1] - centre
    to_south = padded[:, :, :-2, 1:-1] - centre
    flat_zero = jnp.zeros_like(centre[:, :1])
    upper = jnp.concatenate([centre[:, 1:] - centre[:, :-1], flat_zero], axis=1)
    lower = jnp.concatenate([flat_zero, centre[:, :-1] - centre[:, 1:]], axis=1)
    return (
        centre
        + rates[0] * to_east
        + rates[1] * to_west
        + rates[2] * to_north
        + rates[3] * to_south
        + rates[4] * upper
        + rates[5] * lower
    )


def pole_mask(padded, margin, interior):
    band = lax.axis_index("lat")
    last_band = lax.axis_size("lat") - 1
    row_ids = jnp.arange(interior + 2 * margin, dtype=jnp.int32)
    outside = (row_ids < margin) & (band == 0) | (row_ids >= interior + margin) & (
        band == last_band
    )
    return jnp.where(outside[None, None, :, None], 0.0, padded)


def shards(
    adjoint,
    transport,
    cell_weight,
    region_local,
    tile_regions,
    polar_rows,
    week_index,
    grad_in,
    covariance,
):
    tracers, levels, lat_rows, lon_cols = adjoint.shape
    region_count = covariance.shape[1]
    own_rows = covariance.shape[0]
    week_cols = grad_in.shape[1] // tracers
    lon_count = lax.axis_size(LON)
    my_tile = lax.axis_index("lat") * lon_count + lax.axis_index(LON)
    base = jnp.dot(
        covariance,
        lax.all_gather(grad_in, LAT_LON, axis=0, tiled=True),
        preferred_element_type=jnp.float32,
    )
    extended, rate_ext = (
        extended_2(adjoint, (("lat", 2), (LON, 3)), 2),
        extended_2(transport, (("lat", 2), (LON, 3)), 2),
    )
    extended = pole_mask(extended, 2, lat_rows)
    first = advance(extended, rate_ext[:, :, 1:-1, 1:-1])
    first = pole_mask(first, 1, lat_rows)
    field = advance(first, transport)
    row_sums = one_axis_at_a_time(jnp.sum(field, axis=3), LON)
    zonal = row_sums / (lon_cols * lon_count)
    flags = polar_rows.astype(jnp.float32)[None, None, :, None]
    adjoint_out = field + 0.5 * flags * (zonal[..., None] - field)
    surface = (adjoint_out[:, 0] * cell_weight[None]).reshape(tracers, -1)
    local_count = tile_regions.shape[1]
    one_hot = (
        region_local.reshape(1, -1) == jnp.arange(local_count, dtype=jnp.int32)[:, None]
    ).astype(jnp.float32)
    local_sums = lax.dot_general(
        one_hot,
        surface,
        (((1,), (1,)), ((), ())),
        precision=lax.Precision.HIGHEST,
        preferred_element_type=jnp.float32,
    )
    my_regions = lax.dynamic_index_in_dim(tile_regions, my_tile, 0, keepdims=False)
    dense = jnp.zeros((region_count, tracers), jnp.float32).at[my_regions].add(local_sums)
    fresh_all = lax.psum(dense, LAT_LON).astype(jnp.bfloat16)
    added = jnp.dot(covariance, fresh_all, preferred_element_type=jnp.float32)
    week_hot = (jnp.arange(week_cols, dtype=jnp.int32) == week_index[0]).astype(jnp.float32)
    precond = (
        base.reshape(own_rows, week_cols, tracers) + week_hot[None, :, None] * added[:, None, :]
    )
    return (adjoint_out, precond.reshape(own_rows, week_cols * tracers))


def solution(mesh):
    split = Mesh(mesh.devices.reshape(mesh.shape["lat"], 8, 2), ("lat", "lon_0", "lon_1"))
    placed = (
        P(None, None, "lat", LON),
        P(None, None, "lat", LON),
        P("lat", LON),
        P("lat", LON),
        P(),
        P("lat"),
        P(),
        P(LAT_LON, None),
        P(LAT_LON, None),
    )
    return jax.shard_map(
        shards,
        mesh=split,
        in_specs=placed,
        out_specs=(P(None, None, "lat", LON), P(LAT_LON, None)),
        check_vma=False,
    )
```

profile of v0, /device:TPU:96, one launch (start us, length us, event | category | flops | bytes accessed | tf_op | source)
XLA Modules:
  0.0 765.9 jit_solution(8474163198109357353)
XLA Ops:
  7.2 0.0 copy-start
  7.2 0.0 all-gather.2.cloned.1.call-start
  7.2 0.7 all-gather.2.cloned.1.call-update
  7.9 1.1 fusion.36
  9.0 0.1 collective-permute-start.4
  9.1 3.8 collective-permute-start.5
  12.9 1.1 fusion.35
  14.0 0.6 copy.87
  14.7 0.0 collective-permute-start
  14.7 0.6 copy.88
  15.3 3.9 collective-permute-start.1
  19.1 0.7 compare_select_fusion
  19.8 0.7 convert_multiply_fusion
  20.5 2.0 slice_bitcast_fusion.5
  22.5 0.5 and_or_fusion.1
  23.0 3.2 copy.74
  26.8 0.0 collective-permute-done.4
  26.8 2.2 copy.73
  29.0 0.0 collective-permute-done.5
  29.0 2.2 copy.75
  31.2 1.8 pad_maximum_fusion.9
  33.0 3.0 collective-permute-start.6
  36.0 1.4 collective-permute-start.7
  37.4 2.6 copy.69
  40.1 1.9 copy.76
  42.0 1.9 copy.77
  43.9 1.9 copy.78
  45.8 1.0 copy.79
  46.8 1.0 copy.80
  47.8 1.0 copy.81
  48.8 0.1 mul.212
  48.9 0.1 mul.213
  49.0 0.0 collective-permute-done.6
  49.0 0.0 collective-permute-done.7
  49.0 4.4 maximum_bitcast_fusion.4
  53.4 0.0 collective-permute-done
  53.4 3.5 copy.68
  56.9 0.0 collective-permute-done.1
  56.9 3.4 copy.70
  60.3 1.3 pad_maximum_fusion.6
  61.7 2.2 collective-permute-start.2
  63.8 2.3 collective-permute-start.3
  66.2 0.0 copy-done.3
  66.2 3.8 maximum_bitcast_fusion.3
  69.9 0.0 collective-permute-done.2
  69.9 1.3 collective-permute-done.3
  71.3 2.5 maximum_select_fusion
  73.8 4.2 slice_subtract_fusion.9
  78.1 6.4 fusion.4
  84.5 2.2 slice_subtract_fusion.11
  86.8 6.9 fusion.33
  93.7 28.0 %psum.21 = f32[8,8,32]{2,1,0:T(8,128)S(1)} all-reduce(f32[8,8,32]{2,1,0:T(8,128)S(1)} %get-tuple-element.10), channel_id=1, replica_groups=mesh['lat'=16,'lon_0'=8,'lon_1'=2] {'lon_0'}, use_global_device_ids=true, to_apply=%region_1.2 | all-reduce | flops 2048 | bytes 16384 | tf_op jit(solution)/shard_map/psum | solution.py:26
  121.7 12.6 %psum.22 = f32[8,8,32]{2,1,0:T(8,128)S(1)} all-reduce(f32[8,8,32]{2,1,0:T(8,128)S(1)} %psum.21), channel_id=1, replica_groups=mesh['lat'=16,'lon_0'=8,'lon_1'=2] {'lon_1'}, use_global_device_ids=true, to_apply=%region_2.3 | all-reduce | flops 2048 | bytes 16384 | tf_op jit(solution)/shard_map/psum | solution.py:26
  134.3 2.7 multiply_add_fusion
  137.0 1.9 copy-done.7
  138.9 3.8 copy.85
  142.8 0.3 copy.82
  143.1 2.0 fusion.25
  145.0 5.2 scatter_custom_fusion
  150.2 144.0 %all-reduce.5 = bf16[16384,8]{1,0:T(8,128)(2,1)} all-reduce(f32[16384,8]{1,0:T(8,128)} %scatter_custom_fusion), channel_id=1, replica_groups=mesh['lat'=16,'lon_0'=8,'lon_1'=2] {'lat','lon_0','lon_1'}, use_global_device_ids=true, to_apply=%region_4.5 | all-reduce | flops 131072 | bytes 786432 | tf_op jit(solution)/shard_map/psum | solution.py:107
  294.2 3.4 fusion.27
  297.6 0.1 copy.84
  297.8 451.9 %all-gather.2.cloned.1.call-done = bf16[16384,416]{1,0:T(8,128)(2,1)} async-done(((bf16[64,416]{1,0:T(8,128)(2,1)}), bf16[16384,416]{1,0:T(8,128)(2,1)}) %all-gather.2.cloned.1.call-update) | async-done | bytes 13631504 | tf_op jit(solution)/shard_map/all_gather | solution.py:78
  749.6 9.4 %convolution_add_fusion = f32[64,416]{1,0:T(8,128)} fusion(bf16[64,16384]{1,0:T(8,128)(2,1)S(1)} %copy-done, bf16[16384,416]{1,0:T(8,128)(2,1)} %all-gather.2.cloned.1.call-done, f32[64,416]{1,0:T(8,128)S(1)} %copy.84, f32[416]{0:T(512)S(1)} %mul.213), kind=kOutput, calls=%fused_computation.43 | convolution fusion | flops 872468480 | bytes 15943296 | tf_op jit(solution)/shard_map/dot_general | solution.py:76
  (41 shorter events, 0.1 us)
Async XLA Ops:
  7.2 287.0 %copy-start = (bf16[64,16384]{1,0:T(8,128)(2,1)S(1)}, bf16[64,16384]{1,0:T(8,128)(2,1)}, u32[]{:S(2)}) copy-start(bf16[64,16384]{1,0:T(8,128)(2,1)} %param.17) | copy-start | bytes 6291460
  7.2 742.4 %all-gather.2.cloned.1.call-start = ((), (), s32[]{:S(2)}) async-start(), calls=%async_computation | async-start | bytes 16842752 | tf_op jit(solution)/shard_map/all_gather | solution.py:78
  9.0 17.8 %collective-permute-start.4 = (f32[6,8,2,128]{3,1,2,0:T(8,128)S(1)}, f32[6,8,2,128]{3,1,2,0:T(8,128)S(1)}, u32[]{:S(2)}, u32[]{:S(2)}) collective-permute-start(f32[6,8,2,128]{3,1,2,0:T(8,128)S(1)} %copy.89), channel_id=1, source_target_pairs={{0,16},{16,32},{32,48},{48,64},{64,80},{80,96},{96,112},{112,128},... | collective-permute-start | bytes 147464 | tf_op jit(solution)/shard_map/ppermute | solution.py:19
  9.1 19.9 %collective-permute-start.5 = (f32[6,8,2,128]{3,1,2,0:T(8,128)S(1)}, f32[6,8,2,128]{3,1,2,0:T(8,128)S(1)}, u32[]{:S(2)}, u32[]{:S(2)}) collective-permute-start(f32[6,8,2,128]{3,1,2,0:T(8,128)S(1)} %copy.90), channel_id=1, source_target_pairs={{16,0},{32,16},{48,32},{64,48},{80,64},{96,80},{112,96},{128,112},... | collective-permute-start | bytes 147464 | tf_op jit(solution)/shard_map/ppermute | solution.py:20
  14.7 38.8 %collective-permute-start = (f32[8,8,2,128]{3,1,2,0:T(8,128)}, f32[8,8,2,128]{3,1,2,0:T(8,128)}, u32[]{:S(2)}, u32[]{:S(2)}) collective-permute-start(f32[8,8,2,128]{3,1,2,0:T(8,128)} %copy.87), channel_id=1, source_target_pairs={{0,16},{16,32},{32,48},{48,64},{64,80},{80,96},{96,112},{112,128},... | collective-permute-start | bytes 196616 | tf_op jit(solution)/shard_map/ppermute | solution.py:19
  15.3 41.6 %collective-permute-start.1 = (f32[8,8,2,128]{3,1,2,0:T(8,128)}, f32[8,8,2,128]{3,1,2,0:T(8,128)}, u32[]{:S(2)}, u32[]{:S(2)}) collective-permute-start(f32[8,8,2,128]{3,1,2,0:T(8,128)} %copy.88), channel_id=1, source_target_pairs={{16,0},{32,16},{48,32},{64,48},{80,64},{96,80},{112,96},{128,112},... | collective-permute-start | bytes 196616 | tf_op jit(solution)/shard_map/ppermute | solution.py:20
  31.2 6.2 copy-start.14
  33.0 16.0 %collective-permute-start.6 = (f32[6,8,36,2]{2,1,3,0:T(8,128)}, f32[6,8,36,2]{2,1,3,0:T(8,128)}, u32[]{:S(2)}, u32[]{:S(2)}) collective-permute-start(f32[6,8,36,2]{2,1,3,0:T(8,128)} %get-tuple-element.20), channel_id=1, source_target_pairs={{0,1},{1,2},{2,3},{3,4},{4,5},{5,6},{6,7},{7,8},{8,9},{9,10},{10,1... | collective-permute-start | bytes 41480 | tf_op jit(solution)/shard_map/ppermute | solution.py:19
  36.0 13.0 %collective-permute-start.7 = (f32[6,8,36,2]{2,1,3,0:T(8,128)}, f32[6,8,36,2]{2,1,3,0:T(8,128)}, u32[]{:S(2)}, u32[]{:S(2)}) collective-permute-start(f32[6,8,36,2]{2,1,3,0:T(8,128)} %get-tuple-element.21), channel_id=1, source_target_pairs={{1,0},{2,1},{3,2},{4,3},{5,4},{6,5},{7,6},{8,7},{9,8},{10,9},{11,1... | collective-permute-start | bytes 41480 | tf_op jit(solution)/shard_map/ppermute | solution.py:20
  60.3 5.8 copy-start.1
  60.3 5.8 copy-start.2
  60.3 5.8 copy-start.3
  60.3 10.9 %copy-start.6 = (f32[8,8,2,128]{2,1,3,0:T(8,128)S(1)}, f32[8,8,2,128]{2,1,3,0:T(8,128)}, u32[]{:S(2)}) copy-start(f32[8,8,2,128]{2,1,3,0:T(8,128)} %copy.70) | copy-start | bytes 196612
  61.7 8.3 %collective-permute-start.2 = (f32[8,8,36,2]{2,1,3,0:T(8,128)S(1)}, f32[8,8,36,2]{2,1,3,0:T(8,128)S(1)}, u32[]{:S(2)}, u32[]{:S(2)}) collective-permute-start(f32[8,8,36,2]{2,1,3,0:T(8,128)S(1)} %get-tuple-element.12), channel_id=1, source_target_pairs={{0,1},{1,2},{2,3},{3,4},{4,5},{5,6},{6,7},{7,8},{8,9},{9,10},{10,1... | collective-permute-start | bytes 55304 | tf_op jit(solution)/shard_map/ppermute | solution.py:19
  63.8 7.4 copy-start.4
  63.8 7.4 copy-start.5
  63.8 7.4 collective-permute-start.3
  73.8 4.3 copy-start.8
  73.8 4.2 copy-start.15
  84.4 2.3 copy-start.9
  84.4 2.3 copy-start.10
  84.5 2.3 copy-start.11
  84.5 2.3 copy-start.12
  84.5 2.3 copy-start.13
  137.0 1.9 copy-start.7
  138.9 4.1 copy-start.16
  138.9 4.1 copy-start.17
  138.9 3.8 slice-start
Sparse Core Ops, SparseCore 0:
  9.9 739.7 all-gather.1
where the time goes:
time: 767 us; the launch traced here: 766 us
  waiting for transfers between devices  454 us (59%)
  blocking collectives  185 us (24%)
  other arithmetic  43.3 us (6%)
  local copies, waits for them, and re-layouts  37.6 us (5%)
  starting transfers between devices  16.7 us (2%)
  between operations  15 us (2%)
  matrix products  14.8 us (2%)
    all_gather x1, waiting for transfers between devices, shards(): lax.all_gather(grad_in, LAT_LON, axis=0, tiled=True)  452 us
    psum x1, blocking collectives, shards(): fresh_all = lax.psum(dense, LAT_LON).astype(jnp.bfloat16)  144 us
    psum x2, blocking collectives, one_axis_at_a_time(): return functools.reduce(lax.psum, axes, x)  40.6 us
  transfers between devices with their start and end apart: 9, of which 2 were waited for; matrix products, arithmetic and copies ran while one was open for 11% of the time, Pallas kernels for 0%

commit v1 on v0

--- a/solution.py
+++ b/solution.py
@@ -75,7 +75,9 @@
     my_tile = lax.axis_index("lat") * lon_count + lax.axis_index(LON)
     base = jnp.dot(
         covariance,
-        lax.all_gather(grad_in, LAT_LON, axis=0, tiled=True),
+        jnp.concatenate(
+            lax.all_to_all(jnp.stack([grad_in] * lax.axis_size(LAT_LON)), LAT_LON, 0, 0), axis=0
+        ),
         preferred_element_type=jnp.float32,
     )
     extended, rate_ext = (

time: 767 us -> 689 us (0.90); the launches traced: 766 us -> 677 us
  waiting for transfers between devices: 454 us -> 326 us
  local copies, waits for them, and re-layouts: 37.6 us -> 61.4 us
  starting transfers between devices: 16.7 us -> 32.2 us
  matrix products: 14.8 us -> 28.5 us
  between operations: 15 us -> 1.81 us
    all_gather x1 -> x0, waiting for transfers between devices: 452 us -> none  [shards(): lax.all_gather(grad_in, LAT_LON, axis=0, tiled=True)]
    ppermute x4, waiting for transfers between devices: 0.01 us -> 326 us  [extended_2(): before = lax.ppermute(last, axis, up)]
    dot_general x0 -> x1, local copies, waits for them, and re-layouts: none -> 19.6 us  [shards(): jnp.dot(covariance, jnp.concatenate(lax.all_to_all(jnp.stack([grad_in] *...]
    all_to_all x0 -> x1, starting transfers between devices: none -> 15 us  [shards(): lax.all_to_all(jnp.stack([grad_in] * lax.axis_size(LAT_LON)), LAT_LON, 0, 0)]
    dot_general x1, matrix products: 9.43 us -> 23.1 us  [shards(): jnp.dot(covariance, jnp.concatenate(lax.all_to_all(jnp.stack([grad_in] *...]
  transfers between devices with their start and end apart: 9 -> 9, of which waited for: 2 -> 2; matrix products, arithmetic and copies ran while one was open for 11% -> 12% of each run, Pallas kernels for 0% -> 0%
where the time goes in v1:
time: 689 us; the launch traced here: 677 us
  waiting for transfers between devices  326 us (47%)
  blocking collectives  185 us (27%)
  local copies, waits for them, and re-layouts  61.4 us (9%)
  other arithmetic  42 us (6%)
  starting transfers between devices  32.2 us (5%)
  matrix products  28.5 us (4%)
    ppermute x4, waiting for transfers between devices, extended_2(): before = lax.ppermute(last, axis, up)  326 us
    psum x1, blocking collectives, shards(): fresh_all = lax.psum(dense, LAT_LON).astype(jnp.bfloat16)  146 us
    psum x2, blocking collectives, one_axis_at_a_time(): return functools.reduce(lax.psum, axes, x)  39.1 us
    dot_general x1, matrix products, shards(): jnp.dot(covariance, jnp.concatenate(lax.all_to_all(jnp.stack([grad_in] *...  23.1 us
    dot_general x1, local copies, waits for them, and re-layouts, shards(): jnp.dot(covariance, jnp.concatenate(lax.all_to_all(jnp.stack([grad_in] *...  19.6 us
    all_to_all x1, starting transfers between devices, shards(): lax.all_to_all(jnp.stack([grad_in] * lax.axis_size(LAT_LON)), LAT_LON, 0, 0)  15 us
  transfers between devices with their start and end apart: 9, of which 2 were waited for; matrix products, arithmetic and copies ran while one was open for 12% of the time, Pallas kernels for 0%

profile of v1, /device:TPU:96, one launch (start us, length us, event | category | flops | bytes accessed | tf_op | source)
XLA Modules:
  0.0 677.1 jit_solution(11513658782968490787)
XLA Ops:
  0.6 0.0 copy-start
  0.6 6.9 %stack.2 = bf16[256,64,416]{2,1,0:T(8,128)(2,1)} broadcast(bf16[64,416]{1,0:T(8,128)(2,1)} %param.16), dimensions={1,2} | broadcast | bytes 13684736 | tf_op jit(solution)/shard_map/stack | solution.py:79
  7.5 15.0 %all-to-all-start = ((bf16[256,64,416]{2,1,0:T(8,128)(2,1)}), bf16[256,64,416]{2,1,0:T(8,128)(2,1)}, u32[]{:S(2)}, u32[]{:S(2)}) async-start(bf16[256,64,416]{2,1,0:T(8,128)(2,1)} %stack.2), calls=%async_computation | async-start | bytes 33554432 | tf_op jit(solution)/shard_map/all_to_all | solution.py:79
  22.5 0.0 copy-done.8
  22.6 3.6 collective-permute-start.5
  26.2 0.0 collective-permute-start.4
  26.2 1.1 fusion.43
  27.3 0.6 copy.112
  27.9 3.9 collective-permute-start.1
  31.8 0.6 copy.111
  32.4 0.0 collective-permute-start
  32.4 0.7 compare_select_fusion
  33.1 0.0 copy-done.18
  33.1 0.7 slice_bitcast_fusion.5
  33.9 2.2 copy.95
  36.7 27.7 %collective-permute-done.4 = f32[6,8,2,128]{3,1,2,0:T(8,128)S(1)} collective-permute-done((f32[6,8,2,128]{3,1,2,0:T(8,128)S(1)}, f32[6,8,2,128]{3,1,2,0:T(8,128)S(1)}, u32[]{:S(2)}, u32[]{:S(2)}) %collective-permute-start.4) | collective-permute-done | bytes 49184 | tf_op jit(solution)/shard_map/ppermute | solution.py:19
  64.4 2.2 copy.94
  66.6 0.0 collective-permute-done.5
  66.6 2.2 copy.96
  68.8 1.8 pad_maximum_fusion.9
  70.5 4.8 collective-permute-start.6
  75.3 0.0 collective-permute-start.7
  75.3 0.6 compare_convert_fusion
  75.9 2.8 copy.90
  78.7 1.9 copy.97
  80.6 1.9 copy.99
  82.5 1.9 copy.98
  84.4 1.0 copy.100
  85.4 1.0 copy.102
  86.5 1.0 copy.101
  87.5 298.7 %collective-permute-done.6 = f32[6,8,36,2]{2,1,3,0:T(8,128)} collective-permute-done((f32[6,8,36,2]{2,1,3,0:T(8,128)}, f32[6,8,36,2]{2,1,3,0:T(8,128)}, u32[]{:S(2)}, u32[]{:S(2)}) %collective-permute-start.6) | collective-permute-done | bytes 13856 | tf_op jit(solution)/shard_map/ppermute | solution.py:19
  386.2 0.0 collective-permute-done.7
  386.2 4.4 maximum_bitcast_fusion.4
  390.6 0.0 collective-permute-done
  390.6 3.4 copy.89
  394.1 0.0 collective-permute-done.1
  394.1 3.4 copy.91
  397.5 1.3 pad_maximum_fusion.6
  398.8 1.8 collective-permute-start.2
  400.5 3.2 collective-permute-start.3
  403.7 0.0 copy-done.3
  403.7 3.2 maximum_bitcast_fusion.3
  406.9 0.0 collective-permute-done.2
  406.9 0.0 collective-permute-done.3
  406.9 0.0 copy-done.6
  407.0 2.3 maximum_select_fusion
  409.3 4.3 slice_subtract_fusion.9
  413.7 6.3 fusion.6
  420.1 2.2 slice_subtract_fusion.11
  422.4 7.0 %fusion.41 = (f32[8,8,32]{2,1,0:T(8,128)S(1)}, f32[8,8,32,128]{2,1,3,0:T(8,128)}) fusion(f32[8,7,32,128]{2,1,3,0:T(8,128)S(1)} %get-tuple-element.31, f32[8,32,128]{1,0,2:T(8,128)S(1)} %copy-done.14, f32[8,7,32,128]{2,1,3,0:T(8,128)S(1)} %get-tuple-element.30, f32[8,32,128]{1,0,2:T(8,128)} %copy.101, f32[8,8,34,130]{2,1,3,0:T(8,128)S(1)} %fusion.6, ...), kind=kLoop, calls=%fused_computation.80 | loop fusion | flops 4454400 | bytes 8921088 | tf_op jit(solution)/shard_map/reduce_sum | solution.py:91
  429.4 27.7 %psum.21 = f32[8,8,32]{2,1,0:T(8,128)S(1)} all-reduce(f32[8,8,32]{2,1,0:T(8,128)S(1)} %get-tuple-element.16), channel_id=1, replica_groups=mesh['lat'=16,'lon_0'=8,'lon_1'=2] {'lon_0'}, use_global_device_ids=true, to_apply=%region_1.2 | all-reduce | flops 2048 | bytes 16384 | tf_op jit(solution)/shard_map/psum | solution.py:26
  457.1 11.4 %psum.22 = f32[8,8,32]{2,1,0:T(8,128)S(1)} all-reduce(f32[8,8,32]{2,1,0:T(8,128)S(1)} %psum.21), channel_id=1, replica_groups=mesh['lat'=16,'lon_0'=8,'lon_1'=2] {'lon_1'}, use_global_device_ids=true, to_apply=%region_2.3 | all-reduce | flops 2048 | bytes 16384 | tf_op jit(solution)/shard_map/psum | solution.py:26
  468.5 2.6 multiply_add_fusion
  471.1 2.1 copy-done.7
  473.2 3.7 copy.108
  476.9 0.3 copy.105
  477.1 2.0 fusion.27
  479.1 5.2 scatter_custom_fusion
  484.3 145.6 %all-reduce.5 = bf16[16384,8]{1,0:T(8,128)(2,1)} all-reduce(f32[16384,8]{1,0:T(8,128)} %scatter_custom_fusion), channel_id=1, replica_groups=mesh['lat'=16,'lon_0'=8,'lon_1'=2] {'lat','lon_0','lon_1'}, use_global_device_ids=true, to_apply=%region_4.5 | all-reduce | flops 131072 | bytes 786432 | tf_op jit(solution)/shard_map/psum | solution.py:109
  629.9 3.4 fusion.35
  633.3 0.0 all-to-all-done
  633.3 19.6 %copy.103 = bf16[416,16384]{1,0:T(8,128)(2,1)} copy(bf16[416,16384]{0,1:T(8,128)(2,1)} %bitcast.14) | data formatting | bytes 27262976 | tf_op jit(solution)/shard_map/dot_general | solution.py:76
  652.9 23.1 %fusion.30 = f32[64,52,8]{0,1,2:T(8,128)S(1)} fusion(bf16[52,8,16384]{2,1,0:T(8,128)(2,1)} %bitcast.53, bf16[64,16384]{1,0:T(8,128)(2,1)S(1)} %copy-done, f32[64,8]{0,1:T(8,128)S(1)} %fusion.35, f32[52]{0:T(128)S(1)} %copy-done.19), kind=kOutput, calls=%fused_computation.46 | convolution fusion | flops 872468480 | bytes 15837392 | tf_op jit(solution)/shard_map/dot_general | solution.py:76
  676.1 0.8 copy.109
  (44 shorter events, 0.2 us)
Async XLA Ops:
  0.6 629.2 %copy-start = (bf16[64,16384]{1,0:T(8,128)(2,1)S(1)}, bf16[64,16384]{1,0:T(8,128)(2,1)}, u32[]{:S(2)}) copy-start(bf16[64,16384]{1,0:T(8,128)(2,1)} %param.17) | copy-start | bytes 6291460
  7.5 15.0 %copy-start.8 = (f32[6,8,32,128]{3,2,1,0:T(8,128)S(1)}, f32[6,8,32,128]{3,2,1,0:T(8,128)}, u32[]{:S(2)}) copy-start(f32[6,8,32,128]{3,2,1,0:T(8,128)} %param.10) | copy-start | bytes 2359300
  7.5 25.6 %copy-start.18 = (s32[32]{0:T(128)S(1)}, s32[32]{0:T(128)}, u32[]{:S(2)}) copy-start(s32[32]{0:T(128)} %param.14) | copy-start | bytes 388
  7.5 625.8 %all-to-all-start = ((bf16[256,64,416]{2,1,0:T(8,128)(2,1)}), bf16[256,64,416]{2,1,0:T(8,128)(2,1)}, u32[]{:S(2)}, u32[]{:S(2)}) async-start(bf16[256,64,416]{2,1,0:T(8,128)(2,1)} %stack.2), calls=%async_computation | async-start | bytes 33554432 | tf_op jit(solution)/shard_map/all_to_all | solution.py:79
  22.6 44.0 %collective-permute-start.5 = (f32[6,8,2,128]{3,1,2,0:T(8,128)S(1)}, f32[6,8,2,128]{3,1,2,0:T(8,128)S(1)}, u32[]{:S(2)}, u32[]{:S(2)}) collective-permute-start(f32[6,8,2,128]{3,1,2,0:T(8,128)S(1)} %copy.114), channel_id=1, source_target_pairs={{16,0},{32,16},{48,32},{64,48},{80,64},{96,80},{112,96},{128,112},... | collective-permute-start | bytes 147464 | tf_op jit(solution)/shard_map/ppermute | solution.py:20
  26.2 38.2 %collective-permute-start.4 = (f32[6,8,2,128]{3,1,2,0:T(8,128)S(1)}, f32[6,8,2,128]{3,1,2,0:T(8,128)S(1)}, u32[]{:S(2)}, u32[]{:S(2)}) collective-permute-start(f32[6,8,2,128]{3,1,2,0:T(8,128)S(1)} %copy.113), channel_id=1, source_target_pairs={{0,16},{16,32},{32,48},{48,64},{64,80},{80,96},{96,112},{112,128},... | collective-permute-start | bytes 147464 | tf_op jit(solution)/shard_map/ppermute | solution.py:19
  27.9 366.2 %collective-permute-start.1 = (f32[8,8,2,128]{3,1,2,0:T(8,128)}, f32[8,8,2,128]{3,1,2,0:T(8,128)}, u32[]{:S(2)}, u32[]{:S(2)}) collective-permute-start(f32[8,8,2,128]{3,1,2,0:T(8,128)} %copy.112), channel_id=1, source_target_pairs={{16,0},{32,16},{48,32},{64,48},{80,64},{96,80},{112,96},{128,112},... | collective-permute-start | bytes 196616 | tf_op jit(solution)/shard_map/ppermute | solution.py:20
  32.4 358.3 %collective-permute-start = (f32[8,8,2,128]{3,1,2,0:T(8,128)}, f32[8,8,2,128]{3,1,2,0:T(8,128)}, u32[]{:S(2)}, u32[]{:S(2)}) collective-permute-start(f32[8,8,2,128]{3,1,2,0:T(8,128)} %copy.111), channel_id=1, source_target_pairs={{0,16},{16,32},{32,48},{48,64},{64,80},{80,96},{96,112},{112,128},... | collective-permute-start | bytes 196616 | tf_op jit(solution)/shard_map/ppermute | solution.py:19
  68.8 7.2 %copy-start.15 = (f32[8,8,32,128]{3,2,1,0:T(8,128)S(1)}, f32[8,8,32,128]{3,2,1,0:T(8,128)}, u32[]{:S(2)}) copy-start(f32[8,8,32,128]{3,2,1,0:T(8,128)} %param.9) | copy-start | bytes 3145732
  70.5 315.7 %collective-permute-start.6 = (f32[6,8,36,2]{2,1,3,0:T(8,128)}, f32[6,8,36,2]{2,1,3,0:T(8,128)}, u32[]{:S(2)}, u32[]{:S(2)}) collective-permute-start(f32[6,8,36,2]{2,1,3,0:T(8,128)} %get-tuple-element.26), channel_id=1, source_target_pairs={{0,1},{1,2},{2,3},{3,4},{4,5},{5,6},{6,7},{7,8},{8,9},{9,10},{10,1... | collective-permute-start | bytes 41480 | tf_op jit(solution)/shard_map/ppermute | solution.py:19
  75.3 310.9 %collective-permute-start.7 = (f32[6,8,36,2]{2,1,3,0:T(8,128)}, f32[6,8,36,2]{2,1,3,0:T(8,128)}, u32[]{:S(2)}, u32[]{:S(2)}) collective-permute-start(f32[6,8,36,2]{2,1,3,0:T(8,128)} %get-tuple-element.27), channel_id=1, source_target_pairs={{1,0},{2,1},{3,2},{4,3},{5,4},{6,5},{7,6},{8,7},{9,8},{10,9},{11,1... | collective-permute-start | bytes 41480 | tf_op jit(solution)/shard_map/ppermute | solution.py:20
  397.5 6.3 copy-start.1
  397.5 6.3 copy-start.2
  397.5 6.3 copy-start.3
  397.5 9.5 %copy-start.6 = (f32[8,8,2,128]{2,1,3,0:T(8,128)S(1)}, f32[8,8,2,128]{2,1,3,0:T(8,128)}, u32[]{:S(2)}) copy-start(f32[8,8,2,128]{2,1,3,0:T(8,128)} %copy.91) | copy-start | bytes 196612
  398.8 8.2 %collective-permute-start.2 = (f32[8,8,36,2]{2,1,3,0:T(8,128)S(1)}, f32[8,8,36,2]{2,1,3,0:T(8,128)S(1)}, u32[]{:S(2)}, u32[]{:S(2)}) collective-permute-start(f32[8,8,36,2]{2,1,3,0:T(8,128)S(1)} %get-tuple-element.18), channel_id=1, source_target_pairs={{0,1},{1,2},{2,3},{3,4},{4,5},{5,6},{6,7},{7,8},{8,9},{9,10},{10,1... | collective-permute-start | bytes 55304 | tf_op jit(solution)/shard_map/ppermute | solution.py:19
  400.5 6.4 copy-start.4
  400.5 6.4 copy-start.5
  400.5 6.4 collective-permute-start.3
  409.3 4.4 copy-start.9
  420.0 2.3 copy-start.10
  420.0 2.3 copy-start.11
  420.1 2.3 copy-start.12
  420.1 2.3 copy-start.13
  420.1 2.3 copy-start.14
  471.1 2.1 copy-start.7
  473.2 3.9 copy-start.16
  473.2 3.9 copy-start.17
  473.2 3.7 slice-start
  633.3 19.6 %copy-start.19 = (f32[52]{0:T(128)S(1)}, f32[52]{0:T(128)}, u32[]{:S(2)}) copy-start(f32[52]{0:T(128)} %compare_convert_fusion) | copy-start | bytes 628
